TPU v7x, 32 devices: a whole 2x2x4 slice. The times are simulated.
32 devices in a mesh: leaf: 16 (over z, y, core), top: 2 (over x).
Axes of the slice: x: 2, y: 2, z: 4, core: 2. Of those that a mesh axis runs over, the one named last changes fastest.
Arguments:
- vectors: bfloat16 [2, 16, 768, 512], P('top', 'leaf'), may hold values from -6 to 6
- near_tiles: bfloat16 [2, 16, 8, 768, 768], P('top', 'leaf'), may hold values from -0.078125 to 0.078125
- leaf_basis: bfloat16 [2, 16, 768, 128], P('top', 'leaf'), may hold values from -0.21875 to 0.21875
- transfer: bfloat16 [2, 16, 128, 128], P('top', 'leaf'), may hold values from -0.25 to 0.25
- coupling: bfloat16 [2, 16, 7, 128, 128], P('top', 'leaf'), may hold values from -0.1875 to 0.1875
- top_coupling: bfloat16 [2, 2, 128, 128], P('top'), may hold values from -0.375 to 0.375
- near_list: int32 [2, 16, 8], P('top', 'leaf'), may hold values from -4 to 4, as said below
- far_list: int32 [2, 16, 7], P('top', 'leaf'), may hold values from 0 to 15, as said below
- row_counts: int32 [2, 16], P('top', 'leaf'), may hold values from 384 to 768
Outputs:
- product: float32 [2, 16, 768, 512], P('top', 'leaf')
Inputs may be any that keep to these rules, and one draw needn't show every extreme that they name: `near_list`: each leaf's 8 offsets are distinct; an offset that leads outside the cluster's 16 leaves stands for an absent block. `far_list`: each leaf's entries are distinct positions in its cluster, each more than 4 away from the leaf's own position. `row_counts`: rows at and beyond the count are padding.
All inputs are finite; a program needn't handle non-finite values.
Results may differ from a plain program's by a relative error of at most 0.0045.
Values may be sent and summed in bfloat16 or wider, within the bound.
A program may use at most 128 MiB of HBM per device.

v0:
```python
import jax
import jax.numpy as jnp
from jax import lax
from jax.sharding import PartitionSpec as P

REACH = 4


def passed_along(block, axis, distance):
    devices = range(lax.axis_size(axis))
    route = [(i - distance, i) for i in devices if i - distance in devices]
    return lax.ppermute(block, axis, route)


def body(
    vectors,
    near_tiles,
    leaf_basis,
    transfer,
    coupling,
    top_coupling,
    near_list,
    far_list,
    row_counts,
):
    leaf_rows = vectors.shape[2]
    row_index = jnp.arange(leaf_rows, dtype=jnp.int32)
    keep = (row_index < row_counts[0, 0]).astype(jnp.bfloat16)
    masked = vectors[0, 0] * keep[:, None]
    offsets = near_list[0, 0]
    tiles = near_tiles[0, 0]
    window = []
    for offset in range(-REACH, REACH + 1):
        if offset == 0:
            window.append(masked)
        else:
            window.append(passed_along(masked, "leaf", -offset))
    stacked = jnp.stack(window)
    span = jnp.arange(-REACH, REACH + 1, dtype=jnp.int32)
    picker = (offsets[:, None] == span[None, :]).astype(jnp.bfloat16)
    sources = jnp.einsum("kw,wrv->krv", picker, stacked, preferred_element_type=jnp.float32)
    near = jnp.einsum(
        "kij,kjv->iv", tiles, sources.astype(jnp.bfloat16), preferred_element_type=jnp.float32
    )
    basis = leaf_basis[0, 0]
    coeff = jnp.einsum("ir,iv->rv", basis, masked, preferred_element_type=jnp.float32).astype(
        jnp.bfloat16
    )
    nested = transfer[0, 0]
    upward = jnp.einsum("ab,av->bv", nested, coeff, preferred_element_type=jnp.float32)
    clusters = lax.axis_size("top")
    owner = (jnp.arange(clusters, dtype=jnp.int32) == lax.axis_index("top")).astype(jnp.float32)
    parents = lax.psum(owner[:, None, None] * upward[None], ("leaf", "top")).astype(jnp.bfloat16)
    sibling_ids = (lax.axis_index("top") + 1 + jnp.arange(clusters, dtype=jnp.int32)) % clusters
    top_pick = (sibling_ids[:, None] == jnp.arange(clusters, dtype=jnp.int32)[None, :]).astype(
        jnp.bfloat16
    )
    chosen = jnp.einsum(
        "mc,crv->mrv", top_pick, parents, preferred_element_type=jnp.float32
    ).astype(jnp.bfloat16)
    parent_field = jnp.einsum(
        "mab,mbv->av", top_coupling[0], chosen, preferred_element_type=jnp.float32
    ).astype(jnp.bfloat16)
    siblings = far_list[0, 0]
    matrices = coupling[0, 0]
    piece = lax.all_gather(coeff[None], "leaf", axis=0, tiled=True)
    blocks = jnp.arange(piece.shape[0], dtype=jnp.int32)
    chooser = (siblings[:, None] == blocks[None, :]).astype(jnp.bfloat16)
    gathered = jnp.einsum("mn,nrv->mrv", chooser, piece, preferred_element_type=jnp.float32).astype(
        jnp.bfloat16
    )
    local_field = jnp.einsum("mab,mbv->av", matrices, gathered, preferred_element_type=jnp.float32)
    local_field = (
        local_field + jnp.dot(nested, parent_field, preferred_element_type=jnp.float32)
    ).astype(jnp.bfloat16)
    result = near + jnp.dot(basis, local_field, preferred_element_type=jnp.float32)
    result = result * keep[:, None].astype(jnp.float32)
    return result[None, None]


def solution(mesh):
    in_specs = (
        P("top", "leaf", None, None),
        P("top", "leaf", None, None, None),
        P("top", "leaf", None, None),
        P("top", "leaf", None, None),
        P("top", "leaf", None, None, None),
        P("top", None, None, None),
        P("top", "leaf", None),
        P("top", "leaf", None),
        P("top", "leaf"),
    )
    out_specs = P("top", "leaf", None, None)
    return jax.shard_map(body, mesh=mesh, in_specs=in_specs, out_specs=out_specs, check_vma=False)
```

profile of v0, /device:TPU:9, one launch (start us, length us, event | category | flops | bytes accessed | tf_op | source)
XLA Modules:
  0.0 214.7 jit_solution(1711316566224805380)
XLA Ops:
  7.3 1.3 bitcast_multiply_fusion.1
  8.6 3.2 %collective-permute-start = (bf16[768,512]{1,0:T(8,128)(2,1)S(1)}, bf16[768,512]{1,0:T(8,128)(2,1)}, u32[]{:S(2)}, u32[]{:S(2)}) collective-permute-start(bf16[768,512]{1,0:T(8,128)(2,1)S(1)} %bitcast_multiply_fusion.1), channel_id=1, source_target_pairs={{0,8},{2,10},{4,12},{6,14},{8,16},{10,18},{12,20},{14,22},{16,24},... | collective-permute-start | bytes 2359304 | tf_op jit(solution)/shard_map/ppermute | solution.py:12
  11.8 4.0 %collective-permute-start.1 = (bf16[768,512]{1,0:T(8,128)(2,1)S(1)}, bf16[768,512]{1,0:T(8,128)(2,1)}, u32[]{:S(2)}, u32[]{:S(2)}) collective-permute-start(bf16[768,512]{1,0:T(8,128)(2,1)S(1)} %bitcast_multiply_fusion.1), channel_id=1, source_target_pairs={{0,6},{2,8},{4,10},{6,12},{8,14},{10,16},{12,18},{14,20},{16,22},{... | collective-permute-start | bytes 2359304 | tf_op jit(solution)/shard_map/ppermute | solution.py:12
  15.9 3.1 %collective-permute-start.2 = (bf16[768,512]{1,0:T(8,128)(2,1)S(1)}, bf16[768,512]{1,0:T(8,128)(2,1)}, u32[]{:S(2)}, u32[]{:S(2)}) collective-permute-start(bf16[768,512]{1,0:T(8,128)(2,1)S(1)} %bitcast_multiply_fusion.1), channel_id=1, source_target_pairs={{0,4},{2,6},{4,8},{6,10},{8,12},{10,14},{12,16},{14,18},{16,20},{1... | collective-permute-start | bytes 2359304 | tf_op jit(solution)/shard_map/ppermute | solution.py:12
  19.0 2.8 %collective-permute-start.3 = (bf16[768,512]{1,0:T(8,128)(2,1)S(1)}, bf16[768,512]{1,0:T(8,128)(2,1)}, u32[]{:S(2)}, u32[]{:S(2)}) collective-permute-start(bf16[768,512]{1,0:T(8,128)(2,1)S(1)} %bitcast_multiply_fusion.1), channel_id=1, source_target_pairs={{0,2},{2,4},{4,6},{6,8},{8,10},{10,12},{12,14},{14,16},{16,18},{18... | collective-permute-start | bytes 2359304 | tf_op jit(solution)/shard_map/ppermute | solution.py:12
  21.8 1.9 collective-permute-start.4
  23.8 2.4 %convolution_convert_fusion = bf16[512,128]{1,0:T(8,128)(2,1)} fusion(bf16[1,1,768,512]{3,2,1,0:T(8,128)(2,1)} %param.9, bf16[768]{0:T(1024)(128)(2,1)S(1)} %fusion.27, bf16[1,1,768,128]{3,2,1,0:T(8,128)(2,1)} %param.11), kind=kOutput, calls=%fused_computation.15 | convolution fusion | flops 101122048 | bytes 1115648 | tf_op jit(solution)/shard_map/ir,iv->rv/dot_general | solution.py:46
  27.5 84.7 %all-reduce.1 = bf16[2,128,512]{2,1,0:T(8,128)(2,1)S(1)} all-reduce(f32[2,128,512]{2,1,0:T(8,128)S(1)} %broadcast_multiply_fusion), channel_id=1, replica_groups=mesh['leaf'=16,'top'=2] {'leaf','top'}, use_global_device_ids=true, to_apply=%region_0.0 | all-reduce | flops 131072 | bytes 786432 | tf_op jit(solution)/shard_map/psum | solution.py:53
  113.9 2.5 %collective-permute-start.5 = (bf16[768,512]{1,0:T(8,128)(2,1)S(1)}, bf16[768,512]{1,0:T(8,128)(2,1)S(1)}, u32[]{:S(2)}, u32[]{:S(2)}) collective-permute-start(bf16[768,512]{1,0:T(8,128)(2,1)S(1)} %bitcast_multiply_fusion.1), channel_id=1, source_target_pairs={{4,0},{6,2},{8,4},{10,6},{12,8},{14,10},{16,12},{18,14},{20,16},{2... | collective-permute-start | bytes 2359304 | tf_op jit(solution)/shard_map/ppermute | solution.py:12
  117.6 4.8 %collective-permute-start.6 = (bf16[768,512]{1,0:T(8,128)(2,1)S(1)}, bf16[768,512]{1,0:T(8,128)(2,1)S(1)}, u32[]{:S(2)}, u32[]{:S(2)}) collective-permute-start(bf16[768,512]{1,0:T(8,128)(2,1)S(1)} %bitcast_multiply_fusion.1), channel_id=1, source_target_pairs={{6,0},{8,2},{10,4},{12,6},{14,8},{16,10},{18,12},{20,14},{22,16},{... | collective-permute-start | bytes 2359304 | tf_op jit(solution)/shard_map/ppermute | solution.py:12
  122.4 1.2 bitcast_dynamic-update-slice_fusion.6
  123.6 2.1 collective-permute-start.7
  125.7 1.2 bitcast_dynamic-update-slice_fusion.5
  128.4 4.0 %collective-permute-done.5 = bf16[768,512]{1,0:T(8,128)(2,1)S(1)} collective-permute-done((bf16[768,512]{1,0:T(8,128)(2,1)S(1)}, bf16[768,512]{1,0:T(8,128)(2,1)S(1)}, u32[]{:S(2)}, u32[]{:S(2)}) %collective-permute-start.5) | collective-permute-done | bytes 786464 | tf_op jit(solution)/shard_map/ppermute | solution.py:12
  132.5 22.3 %collective-permute-done.6 = bf16[768,512]{1,0:T(8,128)(2,1)S(1)} collective-permute-done((bf16[768,512]{1,0:T(8,128)(2,1)S(1)}, bf16[768,512]{1,0:T(8,128)(2,1)S(1)}, u32[]{:S(2)}, u32[]{:S(2)}) %collective-permute-start.6) | collective-permute-done | bytes 786464 | tf_op jit(solution)/shard_map/ppermute | solution.py:12
  154.9 13.2 %collective-permute-done.7 = bf16[768,512]{1,0:T(8,128)(2,1)S(1)} collective-permute-done((bf16[768,512]{1,0:T(8,128)(2,1)S(1)}, bf16[768,512]{1,0:T(8,128)(2,1)S(1)}, u32[]{:S(2)}, u32[]{:S(2)}) %collective-permute-start.7) | collective-permute-done | bytes 786464 | tf_op jit(solution)/shard_map/ppermute | solution.py:12
  168.1 8.7 %fusion = bf16[8,768,512]{2,0,1:T(8,128)(2,1)} fusion(bf16[9,768,512]{2,1,0:T(8,128)(2,1)S(1)} %bitcast_dynamic-update-slice_fusion, s32[9]{0:T(128)S(1)} %iota_add_fusion, s32[8]{0:T(128)S(1)} %bitcast.91), kind=kOutput, calls=%fused_computation | convolution fusion | flops 56623176 | bytes 13369412 | tf_op jit(solution)/shard_map/kw,wrv->krv/dot_general | solution.py:41
  176.8 9.1 %copy.12 = bf16[8,768,512]{1,2,0:T(8,128)(2,1)} copy(bf16[8,768,512]{2,0,1:T(8,128)(2,1)} %fusion) | data formatting | bytes 12582912 | tf_op jit(solution)/shard_map/kw,wrv->krv/dot_general | solution.py:41
  185.9 2.3 %copy.17 = bf16[64,8,16,128]{3,2,1,0:T(8,128)(2,1)S(1)} copy(bf16[64,8,16,128]{3,1,2,0:T(8,128)(2,1)} %bitcast.89) | data formatting | bytes 4194304
  188.1 3.6 %copy.13 = bf16[16,128,512]{2,0,1:T(8,128)(2,1)} copy(bf16[16,128,512]{1,0,2:T(8,128)(2,1)S(1)} %bitcast.88) | data formatting | bytes 4194304 | tf_op jit(solution)/shard_map/all_gather | solution.py:66
  191.7 2.1 fusion.29
  194.4 1.7 fusion.13
  196.0 10.2 %fusion.6 = f32[1,1,768,512]{2,3,1,0:T(8,128)S(1)} fusion(f32[512,768]{1,0:T(8,128)} %fusion.13, bf16[1,1,8,768,768]{4,3,2,1,0:T(8,128)(2,1)} %param.10, bf16[8,768,512]{1,2,0:T(8,128)(2,1)} %copy.12, f32[768]{0:T(1024)S(1)} %fusion.37), kind=kOutput, calls=%fused_computation.8 | convolution fusion | flops 4832624640 | bytes 18877440 | tf_op jit(solution)/shard_map/kij,kjv->iv/dot_general | solution.py:42
  206.2 1.6 copy.10
  (37 shorter events, 6.3 us)
Async XLA Ops:
  6.5 187.2 %copy-start = (bf16[1,1,7,128,128]{4,3,2,1,0:T(8,128)(2,1)S(1)}, bf16[1,1,7,128,128]{4,3,2,1,0:T(8,128)(2,1)}, u32[]{:S(2)}) copy-start(bf16[1,1,7,128,128]{4,3,2,1,0:T(8,128)(2,1)} %param.13) | copy-start | bytes 688132
  6.5 121.6 %copy-start.1 = (bf16[1,1,768,512]{3,2,1,0:T(8,128)(2,1)S(1)}, bf16[1,1,768,512]{3,2,1,0:T(8,128)(2,1)}, u32[]{:S(2)}) copy-start(bf16[1,1,768,512]{3,2,1,0:T(8,128)(2,1)} %param.9) | copy-start | bytes 2359300
  6.5 179.3 %all-gather.3.cloned.1.call-start = ((), (), s32[]{:S(2)}) async-start(), calls=%async_computation | async-start | bytes 2228224 | tf_op jit(solution)/shard_map/all_gather | solution.py:66
  8.6 105.3 %collective-permute-start = (bf16[768,512]{1,0:T(8,128)(2,1)S(1)}, bf16[768,512]{1,0:T(8,128)(2,1)}, u32[]{:S(2)}, u32[]{:S(2)}) collective-permute-start(bf16[768,512]{1,0:T(8,128)(2,1)S(1)} %bitcast_multiply_fusion.1), channel_id=1, source_target_pairs={{0,8},{2,10},{4,12},{6,14},{8,16},{10,18},{12,20},{14,22},{16,24},... | collective-permute-start | bytes 2359304 | tf_op jit(solution)/shard_map/ppermute | solution.py:12
  11.8 105.8 %collective-permute-start.1 = (bf16[768,512]{1,0:T(8,128)(2,1)S(1)}, bf16[768,512]{1,0:T(8,128)(2,1)}, u32[]{:S(2)}, u32[]{:S(2)}) collective-permute-start(bf16[768,512]{1,0:T(8,128)(2,1)S(1)} %bitcast_multiply_fusion.1), channel_id=1, source_target_pairs={{0,6},{2,8},{4,10},{6,12},{8,14},{10,16},{12,18},{14,20},{16,22},{... | collective-permute-start | bytes 2359304 | tf_op jit(solution)/shard_map/ppermute | solution.py:12
  15.9 107.7 %collective-permute-start.2 = (bf16[768,512]{1,0:T(8,128)(2,1)S(1)}, bf16[768,512]{1,0:T(8,128)(2,1)}, u32[]{:S(2)}, u32[]{:S(2)}) collective-permute-start(bf16[768,512]{1,0:T(8,128)(2,1)S(1)} %bitcast_multiply_fusion.1), channel_id=1, source_target_pairs={{0,4},{2,6},{4,8},{6,10},{8,12},{10,14},{12,16},{14,18},{16,20},{1... | collective-permute-start | bytes 2359304 | tf_op jit(solution)/shard_map/ppermute | solution.py:12
  19.0 107.9 %collective-permute-start.3 = (bf16[768,512]{1,0:T(8,128)(2,1)S(1)}, bf16[768,512]{1,0:T(8,128)(2,1)}, u32[]{:S(2)}, u32[]{:S(2)}) collective-permute-start(bf16[768,512]{1,0:T(8,128)(2,1)S(1)} %bitcast_multiply_fusion.1), channel_id=1, source_target_pairs={{0,2},{2,4},{4,6},{6,8},{8,10},{10,12},{12,14},{14,16},{16,18},{18... | collective-permute-start | bytes 2359304 | tf_op jit(solution)/shard_map/ppermute | solution.py:12
  21.8 106.5 %collective-permute-start.4 = (bf16[768,512]{1,0:T(8,128)(2,1)S(1)}, bf16[768,512]{1,0:T(8,128)(2,1)S(1)}, u32[]{:S(2)}, u32[]{:S(2)}) collective-permute-start(bf16[768,512]{1,0:T(8,128)(2,1)S(1)} %bitcast_multiply_fusion.1), channel_id=1, source_target_pairs={{2,0},{4,2},{6,4},{8,6},{10,8},{12,10},{14,12},{16,14},{18,16},{20... | collective-permute-start | bytes 2359304 | tf_op jit(solution)/shard_map/ppermute | solution.py:12
  113.9 54.2 %copy-start.4 = (s32[1,1,8]{2,1,0:T(1,128)S(1)}, s32[1,1,8]{2,1,0:T(1,128)}, u32[]{:S(2)}) copy-start(s32[1,1,8]{2,1,0:T(1,128)} %param.15) | copy-start | bytes 100
  113.9 18.5 %collective-permute-start.5 = (bf16[768,512]{1,0:T(8,128)(2,1)S(1)}, bf16[768,512]{1,0:T(8,128)(2,1)S(1)}, u32[]{:S(2)}, u32[]{:S(2)}) collective-permute-start(bf16[768,512]{1,0:T(8,128)(2,1)S(1)} %bitcast_multiply_fusion.1), channel_id=1, source_target_pairs={{4,0},{6,2},{8,4},{10,6},{12,8},{14,10},{16,12},{18,14},{20,16},{2... | collective-permute-start | bytes 2359304 | tf_op jit(solution)/shard_map/ppermute | solution.py:12
  117.6 37.2 %collective-permute-start.6 = (bf16[768,512]{1,0:T(8,128)(2,1)S(1)}, bf16[768,512]{1,0:T(8,128)(2,1)S(1)}, u32[]{:S(2)}, u32[]{:S(2)}) collective-permute-start(bf16[768,512]{1,0:T(8,128)(2,1)S(1)} %bitcast_multiply_fusion.1), channel_id=1, source_target_pairs={{6,0},{8,2},{10,4},{12,6},{14,8},{16,10},{18,12},{20,14},{22,16},{... | collective-permute-start | bytes 2359304 | tf_op jit(solution)/shard_map/ppermute | solution.py:12
  123.6 44.5 %collective-permute-start.7 = (bf16[768,512]{1,0:T(8,128)(2,1)S(1)}, bf16[768,512]{1,0:T(8,128)(2,1)S(1)}, u32[]{:S(2)}, u32[]{:S(2)}) collective-permute-start(bf16[768,512]{1,0:T(8,128)(2,1)S(1)} %bitcast_multiply_fusion.1), channel_id=1, source_target_pairs={{8,0},{10,2},{12,4},{14,6},{16,8},{18,10},{20,12},{22,14},{24,16},... | collective-permute-start | bytes 2359304 | tf_op jit(solution)/shard_map/ppermute | solution.py:12
  185.8 5.9 %copy-start.5 = (s32[1,1,7]{2,1,0:T(1,128)S(1)}, s32[1,1,7]{2,1,0:T(1,128)}, u32[]{:S(2)}) copy-start(s32[1,1,7]{2,1,0:T(1,128)} %param.16) | copy-start | bytes 88
  185.8 8.5 %copy-start.2 = (bf16[1,1,768,128]{3,2,1,0:T(8,128)(2,1)S(1)}, bf16[1,1,768,128]{3,2,1,0:T(8,128)(2,1)}, u32[]{:S(2)}) copy-start(bf16[1,1,768,128]{3,2,1,0:T(8,128)(2,1)} %param.11) | copy-start | bytes 589828
  185.8 8.5 %copy-start.3 = (bf16[1,1,128,128]{3,2,1,0:T(8,128)(2,1)S(1)}, bf16[1,1,128,128]{3,2,1,0:T(8,128)(2,1)}, u32[]{:S(2)}) copy-start(bf16[1,1,128,128]{3,2,1,0:T(8,128)(2,1)} %param.12) | copy-start | bytes 98308
Sparse Core Ops, SparseCore 0:
  26.3 52.8 all-gather.2
where the time goes:
time: 218 us; the launch traced here: 215 us
  blocking collectives  84.7 us (39%)
  waiting for transfers between devices  39.6 us (18%)
  matrix products  28.3 us (13%)
  starting transfers between devices  24.5 us (11%)
  local copies, waits for them, and re-layouts  21.5 us (10%)
  between operations  14.4 us (7%)
    psum x1, blocking collectives, body(): lax.psum(owner[:, None, None] * upward[None], ('leaf', 'top'))  84.7 us
    ppermute x8, waiting for transfers between devices, passed_along(): return lax.ppermute(block, axis, route)  39.5 us
    ppermute x8, starting transfers between devices, passed_along(): return lax.ppermute(block, axis, route)  24.5 us
    dot_general x1, matrix products, body(): jnp.einsum('kij,kjv->iv', tiles, sources.astype(jnp.bfloat16), preferred_...  10.2 us
    dot_general x1, local copies, waits for them, and re-layouts, body(): jnp.einsum('kw,wrv->krv', picker, stacked, preferred_element_type=jnp.flo...  9.06 us
    dot_general x1, matrix products, body(): jnp.einsum('kw,wrv->krv', picker, stacked, preferred_element_type=jnp.flo...  8.66 us
    unnamed x20, local copies, waits for them, and re-layouts  7.17 us
  transfers between devices with their start and end apart: 9, of which 3 were waited for; matrix products, arithmetic and copies ran while one was open for 13% of the time, Pallas kernels for 0%

commit v1 on v0

v1 whole, which is shorter than its diff:
```python
import functools

import jax
import jax.numpy as jnp
from jax import lax
from jax.experimental import pallas as pl
from jax.experimental.pallas import tpu as pltpu
from jax.sharding import PartitionSpec as P

REACH = 4


def mirrored(index, bits):
    total = 0
    for bit in range(bits):
        total = total + lax.rem(lax.div(index, 1 << bit), 2) * (1 << (bits - 1 - bit))
    return total


def kernel(
    leaves,
    clusters,
    masked_ref,
    packed_ref,
    window,
    gathered,
    parents,
    send_sem,
    recv_sem,
    step_send,
    step_recv,
    top_send,
    top_recv,
    own_sem,
    same_sem,
):
    me = lax.axis_index("leaf")
    cluster = lax.axis_index("top")
    core = lax.rem(me, 2)
    toward = 1 - 2 * core
    partner = me + toward
    bits = leaves.bit_length() - 1
    vecs = masked_ref.shape[1]
    rank = packed_ref.shape[0]
    spot = mirrored(me, bits)

    own = pltpu.make_async_copy(
        packed_ref, gathered.at[pl.ds(pl.multiple_of(spot * rank, rank), rank)], own_sem
    )
    own.start()
    same = pltpu.make_async_copy(masked_ref, window.at[REACH], same_sem)
    same.start()

    def inside(offset):
        return jnp.logical_and(me + offset >= 0, me + offset < leaves)

    def peer_of(step):
        stride = leaves >> (step + 1)
        return me + stride * (1 - 2 * lax.rem(lax.div(me, stride), 2))

    barrier = pltpu.get_barrier_semaphore()
    expected = bits + clusters - 1
    for offset in (2, -2, 4, -4):
        expected = expected + inside(offset).astype(jnp.int32)

        @pl.when(inside(offset))
        def _(offset=offset):
            pl.semaphore_signal(
                barrier, inc=1, device_id={"leaf": me + offset}, device_id_type=pl.DeviceIdType.MESH
            )

    for step in range(bits):
        pl.semaphore_signal(
            barrier, inc=1, device_id={"leaf": peer_of(step)}, device_id_type=pl.DeviceIdType.MESH
        )
    for shift in range(1, clusters):
        pl.semaphore_signal(
            barrier,
            inc=1,
            device_id={"top": lax.rem(cluster + shift, clusters)},
            device_id_type=pl.DeviceIdType.MESH,
        )
    pl.semaphore_wait(barrier, expected)

    def exchange(step):
        size = 1 << step
        start = lax.div(spot, size) * size
        block = gathered.at[pl.ds(pl.multiple_of(start * rank, rank), size * rank)]
        return pltpu.make_async_remote_copy(
            src_ref=block,
            dst_ref=block,
            send_sem=step_send.at[step],
            recv_sem=step_recv.at[step],
            device_id={"leaf": peer_of(step)},
            device_id_type=pl.DeviceIdType.MESH,
        )

    def direct(offset):
        return pltpu.make_async_remote_copy(
            src_ref=masked_ref,
            dst_ref=window.at[REACH - offset],
            send_sem=send_sem.at[REACH + offset],
            recv_sem=recv_sem.at[REACH - offset],
            device_id={"leaf": me + offset},
            device_id_type=pl.DeviceIdType.MESH,
        )

    def forward(offset, slot):
        return pltpu.make_async_remote_copy(
            src_ref=masked_ref if offset == 0 else window.at[REACH + offset],
            dst_ref=window.at[REACH + offset - toward],
            send_sem=send_sem.at[slot],
            recv_sem=recv_sem.at[REACH + offset - toward],
            device_id={"leaf": partner},
            device_id_type=pl.DeviceIdType.MESH,
        )

    def forwarded(offset):
        if offset == 4:
            return jnp.logical_and(inside(offset), core == 0)
        if offset == -4:
            return jnp.logical_and(inside(offset), core == 1)
        return inside(offset)

    slot_of = {0: 1, 2: 3, -2: 5, 4: 7, -4: 4}

    def arrival(offset):
        block = window.at[REACH + offset]
        return pltpu.make_async_remote_copy(
            src_ref=block,
            dst_ref=block,
            send_sem=send_sem.at[REACH + offset],
            recv_sem=recv_sem.at[REACH + offset],
            device_id={"leaf": partner},
            device_id_type=pl.DeviceIdType.MESH,
        )

    own.wait()
    exchange(0).start()
    forward(0, slot_of[0]).start()
    for offset in (2, -2):

        @pl.when(inside(offset))
        def _(offset=offset):
            direct(offset).start()

    exchange(0).wait_recv()
    exchange(1).start()
    for offset in (4, -4):

        @pl.when(inside(offset))
        def _(offset=offset):
            direct(offset).start()

    exchange(1).wait_recv()
    exchange(2).start()
    for offset in (2, -2):

        @pl.when(inside(offset))
        def _(offset=offset):
            direct(-offset).wait_recv()
            forward(offset, slot_of[offset]).start()

    for step in range(2, bits):
        exchange(step).wait_recv()
        if step + 1 < bits:
            exchange(step + 1).start()

    def contract(left, right):
        return lax.dot_general(
            left, right, (((0,), (0,)), ((), ())), preferred_element_type=jnp.float32
        )

    parent = contract(gathered[:, vecs:], gathered[:, :vecs]).astype(jnp.bfloat16)
    parents[cluster] = parent

    for offset in (4, -4):

        @pl.when(inside(offset))
        def _(offset=offset):
            direct(-offset).wait_recv()

        @pl.when(forwarded(offset))
        def _(offset=offset):
            forward(offset, slot_of[offset]).start()

    def share(shift):
        return pltpu.make_async_remote_copy(
            src_ref=parents.at[cluster],
            dst_ref=parents.at[cluster],
            send_sem=top_send.at[shift],
            recv_sem=top_recv.at[shift],
            device_id={"top": lax.rem(cluster + shift, clusters)},
            device_id_type=pl.DeviceIdType.MESH,
        )

    for shift in range(1, clusters):
        share(shift).start()

    for offset in (1, -1, 3, -3):

        @pl.when(inside(offset))
        def _(offset=offset):
            arrival(offset).wait_recv()

    for shift in range(1, clusters):
        share(shift).wait_recv()
    same.wait()
    for step in range(bits):
        exchange(step).wait_send()
    for shift in range(1, clusters):
        share(shift).wait_send()
    for offset in (2, -2, 4, -4):

        @pl.when(inside(offset))
        def _(offset=offset):
            direct(offset).wait_send()

    for offset in (0, 2, -2, 4, -4):

        @pl.when(forwarded(offset))
        def _(offset=offset):
            forward(offset, slot_of[offset]).wait_send()


def local_kernel(
    clusters,
    slots,
    valid,
    places,
    scalars,
    tile_ref,
    source_ref,
    gathered,
    parents,
    basis_ref,
    nested_ref,
    coupling_ref,
    top_ref,
    out_ref,
):
    k = pl.program_id(0)
    rows, vecs = out_ref.shape
    rank = nested_ref.shape[0]
    part = rows // 3 if rows % 3 == 0 else rows

    @pl.when(k == 0)
    def _():
        out_ref[...] = jnp.zeros_like(out_ref)

    @pl.when(valid[k] == 1)
    def _():
        def piece(index, carry):
            span = pl.ds(pl.multiple_of(index * part, part), part)
            out_ref[span, :] += jnp.dot(
                tile_ref[0, span, :], source_ref[0], preferred_element_type=jnp.float32
            )
            return carry

        lax.fori_loop(0, rows // part, piece, 0)

    @pl.when(k == pl.num_programs(0) - 1)
    def _():
        field = jnp.zeros((rank, vecs), jnp.float32)
        for m in range(coupling_ref.shape[0]):
            start = pl.multiple_of(places[m] * rank, rank)
            field = field + jnp.dot(
                coupling_ref[m],
                gathered[pl.ds(start, rank), :vecs],
                preferred_element_type=jnp.float32,
            )
        above = jnp.zeros((rank, vecs), jnp.float32)
        for m in range(top_ref.shape[0]):
            above = above + jnp.dot(
                top_ref[m],
                parents[lax.rem(scalars[1] + 1 + m, clusters)],
                preferred_element_type=jnp.float32,
            )
        field = field + jnp.dot(
            nested_ref[...], above.astype(jnp.bfloat16), preferred_element_type=jnp.float32
        )
        far = jnp.dot(
            basis_ref[...], field.astype(jnp.bfloat16), preferred_element_type=jnp.float32
        )
        row = lax.broadcasted_iota(jnp.int32, (rows, vecs), 0)
        out_ref[...] = jnp.where(row < scalars[0], out_ref[...] + far, 0.0)


def body(
    vectors,
    near_tiles,
    leaf_basis,
    transfer,
    coupling,
    top_coupling,
    near_list,
    far_list,
    row_counts,
):
    leaves = lax.axis_size("leaf")
    clusters = lax.axis_size("top")
    rows, vecs = vectors.shape[2:]
    keep = (jnp.arange(rows, dtype=jnp.int32) < row_counts[0, 0]).astype(jnp.bfloat16)
    masked = vectors[0, 0] * keep[:, None]
    basis = leaf_basis[0, 0]
    nested = transfer[0, 0]
    rank = nested.shape[0]
    coeff = jnp.einsum("ir,iv->rv", basis, masked, preferred_element_type=jnp.float32).astype(
        jnp.bfloat16
    )
    packed = jnp.concatenate([coeff, nested], axis=1)
    tiles = near_tiles[0, 0]
    bits = leaves.bit_length() - 1
    span = 2 * REACH + 1
    vmem = pl.BlockSpec(memory_space=pltpu.VMEM)
    window, gathered, parents = pl.pallas_call(
        functools.partial(kernel, leaves, clusters),
        out_shape=(
            jax.ShapeDtypeStruct((span, rows, vecs), jnp.bfloat16),
            jax.ShapeDtypeStruct((leaves * rank, vecs + rank), jnp.bfloat16),
            jax.ShapeDtypeStruct((clusters, rank, vecs), jnp.bfloat16),
        ),
        in_specs=[vmem, vmem],
        out_specs=(pl.BlockSpec(memory_space=pl.ANY), vmem, vmem),
        scratch_shapes=[
            pltpu.SemaphoreType.DMA((span,)),
            pltpu.SemaphoreType.DMA((span,)),
            pltpu.SemaphoreType.DMA((bits,)),
            pltpu.SemaphoreType.DMA((bits,)),
            pltpu.SemaphoreType.DMA((clusters,)),
            pltpu.SemaphoreType.DMA((clusters,)),
            pltpu.SemaphoreType.DMA,
            pltpu.SemaphoreType.DMA,
        ],
        compiler_params=pltpu.CompilerParams(
            collective_id=0, has_side_effects=True, vmem_limit_bytes=24 * 1024 * 1024
        ),
        cost_estimate=pl.CostEstimate(
            flops=2 * leaves * rank * rank * vecs,
            bytes_accessed=16 * span * rows * vecs,
            transcendentals=0,
        ),
    )(masked, packed)
    me = lax.axis_index("leaf")
    offsets = near_list[0, 0]
    valid = (me + offsets >= 0) & (me + offsets < leaves)
    slots = jnp.where(valid, offsets + REACH, REACH)
    places = mirrored(far_list[0, 0], bits)
    scalars = jnp.stack([row_counts[0, 0], lax.axis_index("top")]).astype(jnp.int32)

    def whole(array):
        return pl.BlockSpec(array.shape, lambda k, *_: (0,) * array.ndim)

    rest = (gathered, parents, basis, nested, coupling[0, 0], top_coupling[0])
    result = pl.pallas_call(
        functools.partial(local_kernel, clusters),
        out_shape=jax.ShapeDtypeStruct((rows, vecs), jnp.float32),
        grid_spec=pltpu.PrefetchScalarGridSpec(
            num_scalar_prefetch=4,
            grid=(tiles.shape[0],),
            in_specs=[
                pl.BlockSpec((1, rows, rows), lambda k, *_: (k, 0, 0)),
                pl.BlockSpec((1, rows, vecs), lambda k, slots, *_: (slots[k], 0, 0)),
            ]
            + [whole(array) for array in rest],
            out_specs=pl.BlockSpec((rows, vecs), lambda k, *_: (0, 0)),
        ),
        compiler_params=pltpu.CompilerParams(
            dimension_semantics=("arbitrary",), vmem_limit_bytes=32 * 1024 * 1024
        ),
    )(slots, valid.astype(jnp.int32), places, scalars, tiles, window, *rest)
    return result[None, None]


def solution(mesh):
    in_specs = (
        P("top", "leaf", None, None),
        P("top", "leaf", None, None, None),
        P("top", "leaf", None, None),
        P("top", "leaf", None, None),
        P("top", "leaf", None, None, None),
        P("top", None, None, None),
        P("top", "leaf", None),
        P("top", "leaf", None),
        P("top", "leaf"),
    )
    out_specs = P("top", "leaf", None, None)
    return jax.shard_map(body, mesh=mesh, in_specs=in_specs, out_specs=out_specs, check_vma=False)
```

time: 218 us -> 86.6 us (0.40); the launches traced: 215 us -> 86.1 us
  blocking collectives: 84.7 us -> 0 us
  Pallas kernels: 0 us -> 72.6 us
  waiting for transfers between devices: 39.6 us -> 0 us
  matrix products: 28.3 us -> 1.58 us
  starting transfers between devices: 24.5 us -> 0 us
  local copies, waits for them, and re-layouts: 21.5 us -> 7.14 us
  between operations: 14.4 us -> 0.69 us
  other arithmetic: 1.67 us -> 4.15 us
    psum x1 -> x0, blocking collectives: 84.7 us -> none  [body(): lax.psum(owner[:, None, None] * upward[None], ('leaf', 'top'))]
    pallas_call x0 -> x2, Pallas kernels: none -> 72.6 us  [the longest x1 60.7 us: body(): pl.pallas_call(functools.partial(kernel, leaves, clusters), out_shape=(ja...]
    ppermute x8 -> x0, waiting for transfers between devices: 39.5 us -> none  [passed_along(): return lax.ppermute(block, axis, route)]
    dot_general x8 -> x0, matrix products: 25.9 us -> none  [the longest x1 10.2 us: body(): jnp.einsum('kij,kjv->iv', tiles, sources.astype(jnp.bfloat16), preferred_...]
    ppermute x8 -> x0, starting transfers between devices: 24.5 us -> none  [passed_along(): return lax.ppermute(block, axis, route)]
    dot_general x1 -> x0, local copies, waits for them, and re-layouts: 9.06 us -> none  [body(): jnp.einsum('kw,wrv->krv', picker, stacked, preferred_element_type=jnp.flo...]
    all_gather x1 -> x0, local copies, waits for them, and re-layouts: 3.56 us -> none  [body(): piece = lax.all_gather(coeff[None], 'leaf', axis=0, tiled=True)]
    unnamed x20 -> x10, local copies, waits for them, and re-layouts: 7.17 us -> 7.14 us
  transfers between devices with their start and end apart: 9 -> 0, of which waited for: 3 -> 0; matrix products, arithmetic and copies ran while one was open for 13% -> 0% of each run, Pallas kernels for 0% -> 0%
where the time goes in v1:
time: 86.6 us; the launch traced here: 86.1 us
  Pallas kernels  72.6 us (84%)
  local copies, waits for them, and re-layouts  7.14 us (8%)
  other arithmetic  4.15 us (5%)
  matrix products  1.58 us (2%)
    pallas_call x1, Pallas kernels, body(): pl.pallas_call(functools.partial(kernel, leaves, clusters), out_shape=(ja...  60.7 us
    pallas_call x1, Pallas kernels, body(): pl.pallas_call(functools.partial(local_kernel, clusters), out_shape=jax.S...  11.8 us
    unnamed x10, local copies, waits for them, and re-layouts  7.14 us

profile of v1, /device:TPU:9, one launch (start us, length us, event | category | flops | bytes accessed | tf_op | source)
XLA Modules:
  0.0 86.1 jit_solution(17156552667097526076)
XLA Ops:
  0.7 0.1 pad_add_fusion.scalars
  0.7 0.7 fusion.10.places
  1.4 0.7 select_bitcast_fusion.slots
  2.1 0.7 convert_bitcast_fusion.valid
  2.7 1.6 %fusion = bf16[128,512]{1,0:T(8,128)(2,1)S(1)} fusion(bf16[1,1,768,512]{3,2,1,0:T(8,128)(2,1)} %param.9, bf16[768]{0:T(1024)(128)(2,1)S(1)} %fusion.4, bf16[1,1,768,128]{3,2,1,0:T(8,128)(2,1)} %param.11), kind=kOutput, calls=%fused_computation.1 | convolution fusion | flops 101122048 | bytes 1115648 | tf_op jit(solution)/shard_map/ir,iv->rv/dot_general | solution.py:308
  4.3 0.8 pad_maximum_fusion.packed_ref
  5.1 1.3 %bitcast_multiply_fusion.masked_ref = bf16[768,512]{1,0:T(8,128)(2,1)S(1)} fusion(bf16[1,1,768,512]{3,2,1,0:T(8,128)(2,1)} %param.9, bf16[768]{0:T(1024)(128)(2,1)S(1)} %fusion.4), kind=kLoop, calls=%fused_computation.3 | loop fusion | flops 393216 | bytes 1574400 | tf_op jit(solution)/shard_map/mul | solution.py:304
  6.4 60.7 %shard_map.91 = (bf16[9,768,512]{2,1,0:T(8,128)(2,1)S(1)}, bf16[2048,640]{1,0:T(8,128)(2,1)S(1)}, bf16[2,128,512]{2,1,0:T(8,128)(2,1)S(1)}) custom-call(bf16[768,512]{1,0:T(8,128)(2,1)S(1)} %bitcast_multiply_fusion.masked_ref, bf16[128,640]{1,0:T(8,128)(2,1)S(1)} %pad_maximum_fusion.packed_ref), custom_call_target="tpu_custom_call" | custom-call | flops 268435456 | bytes 56623104 | tf_op jit(solution)/shard_map/pallas_call | solution.py:316
  67.1 0.0 copy-start
  67.2 3.7 %copy-done = bf16[1,1,8,768,768]{4,3,2,1,0:T(8,128)(2,1)S(1)} copy-done((bf16[1,1,8,768,768]{4,3,2,1,0:T(8,128)(2,1)S(1)}, bf16[1,1,8,768,768]{4,3,2,1,0:T(8,128)(2,1)}, u32[]{:S(2)}) %copy-start) | copy-done | bytes 9437208
  70.8 0.0 copy-start.1
  70.8 0.9 %copy-done.1 = bf16[1,1,7,128,128]{4,3,2,1,0:T(8,128)(2,1)S(1)} copy-done((bf16[1,1,7,128,128]{4,3,2,1,0:T(8,128)(2,1)S(1)}, bf16[1,1,7,128,128]{4,3,2,1,0:T(8,128)(2,1)}, u32[]{:S(2)}) %copy-start.1) | copy-done | bytes 229400
  71.8 0.0 copy-start.2
  71.8 0.9 %copy-done.2 = bf16[1,1,768,128]{3,2,1,0:T(8,128)(2,1)S(1)} copy-done((bf16[1,1,768,128]{3,2,1,0:T(8,128)(2,1)S(1)}, bf16[1,1,768,128]{3,2,1,0:T(8,128)(2,1)}, u32[]{:S(2)}) %copy-start.2) | copy-done | bytes 196632
  72.7 0.0 copy-start.3
  72.7 0.8 copy-done.3
  73.4 0.0 copy-start.4
  73.5 0.8 copy-done.4
  74.3 11.8 %shard_map.92 = f32[768,512]{1,0:T(8,128)} custom-call(s32[8]{0:T(128)S(1)} %select_bitcast_fusion.slots, s32[8]{0:T(128)S(1)} %convert_bitcast_fusion.valid, s32[7]{0:T(128)S(1)} %fusion.10.places, s32[2]{0:T(128)S(1)} %pad_add_fusion.scalars, bf16[8,768,768]{2,1,0:T(8,128)(2,1)S(1)} %bitcast.37, bf16[9,768,512]{2,1,0:T(8,128)(2,1)S(1)} %get-tuple-element.8.source_ref, ...), custom_call_target="tpu_custom_call" | custom-call | tf_op jit(solution)/shard_map/pallas_call | solution.py:355
  (1 shorter events, 0.0 us)
Async XLA Ops:
  67.1 3.7 %copy-start = (bf16[1,1,8,768,768]{4,3,2,1,0:T(8,128)(2,1)S(1)}, bf16[1,1,8,768,768]{4,3,2,1,0:T(8,128)(2,1)}, u32[]{:S(2)}) copy-start(bf16[1,1,8,768,768]{4,3,2,1,0:T(8,128)(2,1)} %param.10) | copy-start | bytes 28311556
  70.8 0.9 %copy-start.1 = (bf16[1,1,7,128,128]{4,3,2,1,0:T(8,128)(2,1)S(1)}, bf16[1,1,7,128,128]{4,3,2,1,0:T(8,128)(2,1)}, u32[]{:S(2)}) copy-start(bf16[1,1,7,128,128]{4,3,2,1,0:T(8,128)(2,1)} %param.13) | copy-start | bytes 688132
  71.8 0.9 %copy-start.2 = (bf16[1,1,768,128]{3,2,1,0:T(8,128)(2,1)S(1)}, bf16[1,1,768,128]{3,2,1,0:T(8,128)(2,1)}, u32[]{:S(2)}) copy-start(bf16[1,1,768,128]{3,2,1,0:T(8,128)(2,1)} %param.11) | copy-start | bytes 589828
  72.7 0.8 copy-start.3
  73.4 0.8 copy-start.4
